TPU v7x, 32 devices: a whole 2x2x4 slice. The times are simulated.
32 devices in a mesh: groups: 2 (over y), assets: 8 (over z, x), tm: 2 (over core).
Axes of the slice: x: 2, y: 2, z: 4, core: 2. Of those that a mesh axis runs over, the one named last changes fastest.
Arguments:
- returns: bfloat16 [1536, 16384], P('tm', ('groups', 'assets')), parts along dimension 1, may hold values from -24 to 24
- prior: float32 [16384, 8192], P(('groups', 'assets')), parts along dimension 0, may hold values from -3 to 3
Outputs:
- covariance: float32 [2, 16384, 8192], P('tm', ('groups', 'assets')), parts along dimension 1
There are 2 independent parts, one for each index of `groups`. A program takes and returns all parts, laid end to end along the dimension named above; each array names one. Nothing has to cross between parts.
All inputs are finite; a program needn't handle non-finite values.
Results may differ from a plain program's by a relative error of at most 0.0045.
Values may be sent and summed in bfloat16 or wider, within the bound.
A program may use at most 256 MiB of HBM per device.

v0:
```python
import jax
import jax.numpy as jnp
from jax import lax
from jax.sharding import PartitionSpec as P


def prefix(shard, axis, combine, identity):
    length, mine = (lax.axis_size(axis), lax.axis_index(axis))
    everything = jax.tree.map(
        lambda part, kind: lax.all_gather(part.astype(kind), axis),
        shard,
        (jnp.bfloat16, jnp.bfloat16),
    )
    start = jax.tree.map(
        lambda part, zero: jnp.broadcast_to(jnp.asarray(zero, part.dtype), part.shape),
        shard,
        identity,
    )

    def turn(k, before):
        reached = k < mine
        new = combine(
            before, jax.tree.map(lambda part, own: part[k].astype(own.dtype), everything, shard)
        )
        return jax.tree.map(lambda a, b: jnp.where(reached, a, b), new, before)

    return lax.fori_loop(0, length, turn, start)


def cross_tile(left, right):
    return lax.dot_general(
        left, right, (((0,), (0,)), ((), ())), preferred_element_type=jnp.float32
    )


def combine_carry(earlier, later):
    return (later[1] * earlier[0] + later[0], earlier[1] * later[1])


def local(returns, prior):
    minutes, width = returns.shape
    lam = jnp.float32(0.9995)
    position = jnp.arange(minutes, dtype=jnp.float32)
    weight = jnp.sqrt(
        (jnp.float32(1.0) - lam) * jnp.power(lam, jnp.float32(minutes - 1) - position)
    )
    factor = jnp.power(lam, jnp.float32(minutes))
    scaled = (returns.astype(jnp.float32) * weight[:, None]).astype(jnp.bfloat16)
    tile = cross_tile(scaled, lax.all_gather(scaled, "assets", axis=1, tiled=True))
    decay = jnp.full((1,), factor, jnp.float32)
    identity = (jnp.zeros_like(tile), jnp.ones((1,), jnp.float32))
    before, reach = prefix((tile, decay), "tm", combine_carry, identity)
    result = factor * (before + reach[0] * prior) + tile
    return result[None]


def solution(mesh):
    placed = (P("tm", ("groups", "assets")), P(("groups", "assets"), None))
    return jax.shard_map(
        local,
        mesh=mesh,
        in_specs=placed,
        out_specs=P("tm", ("groups", "assets"), None),
        check_vma=False,
    )
```

profile of v0, /device:TPU:0, one launch (start us, length us, event | category | flops | bytes accessed | tf_op | source)
XLA Modules:
  0.0 360.6 jit_solution(16871190527637498569)
XLA Ops:
  6.5 0.0 all-gather.4.cloned.1.call-start
  6.6 2.9 multiply_convert_fusion
  9.5 0.0 all-gather.4.cloned.1.call-update
  9.5 0.0 copy-start
  9.5 0.0 all-gather.6.cloned.1.call-start
  9.6 178.9 %all-gather.4.cloned.1.call-done = bf16[768,8192]{1,0:T(8,128)(2,1)} async-done(((bf16[768,1024]{1,0:T(8,128)(2,1)}), bf16[768,8192]{1,0:T(8,128)(2,1)}) %all-gather.4.cloned.1.call-update) | async-done | bytes 12582928 | tf_op jit(solution)/shard_map/all_gather | solution.py:49
  188.5 24.6 %fusion.1 = (bf16[1024,8192]{1,0:T(8,128)(2,1)}, f32[1024,8192]{1,0:T(8,128)}) fusion(bf16[768,1024]{1,0:T(8,128)(2,1)} %multiply_convert_fusion, bf16[768,8192]{1,0:T(8,128)(2,1)} %all-gather.4.cloned.1.call-done), kind=kOutput, calls=%fused_computation.6 | convolution fusion | flops 12893290496 | bytes 64487424 | tf_op jit(solution)/shard_map/dot_general | solution.py:31
  213.1 0.0 all-gather.6.cloned.1.call-update
  213.1 0.0 copy-done
  213.1 0.6 dynamic-slice
  213.7 0.7 dynamic-update-slice
  214.4 2.4 all-reduce
  216.9 45.6 %all-gather.6.cloned.1.call-done = bf16[2048,8192]{1,0:T(8,128)(2,1)} async-done(((bf16[1024,8192]{1,0:T(8,128)(2,1)}), bf16[2048,8192]{1,0:T(8,128)(2,1)}) %all-gather.6.cloned.1.call-update) | async-done | bytes 33554448 | tf_op jit(solution)/shard_map/all_gather | solution.py:10
  262.4 48.2 %while.16 = (s32[]{:T(128)}, f32[1024,8192]{1,0:T(8,128)}, f32[1]{0:T(128)}, s32[]{:T(128)}, bf16[2,1]{0,1:T(2,128)(2,1)S(1)}, /*index=5*/bf16[2,1024,8192]{2,1,0:T(8,128)(2,1)}, s32[]{:T(128)}, s32[]{:T(128)}) while((s32[]{:T(128)}, f32[1024,8192]{1,0:T(8,128)}, f32[1]{0:T(128)}, s32[]{:T(128)}, bf16[2,1]{0,1:T(2,128)(2,1)S(1)}, ...), condition=%wide.region_1.2_spmd.clone, body=%wide.region_0.1_spmd.clone.sunk | while | flops 41943044 | bytes 83886232 | solution.py:27
  262.4 0.6 constant_dynamic-slice_fusion.2
  263.6 18.9 %fusion.5 = f32[1024,8192]{1,0:T(8,128)} fusion(f32[1024,8192]{1,0:T(8,128)} %get-tuple-element.204, bf16[2,1024,8192]{2,1,0:T(8,128)(2,1)} %get-tuple-element.216, s32[]{:T(128)} %get-tuple-element.203, f32[]{:T(128)} %bitcast.22, pred[]{:T(512)S(6)} %compare.3, pred[]{:T(512)} %lt.22), kind=kLoop, calls=%fused_computation.1.clone.1 | loop fusion | flops 41943040 | bytes 83886088 | tf_op jit(solution)/shard_map/while/body/eval_jaxpr/jit(_where)/select_n | solution.py:25
  282.4 0.6 constant_dynamic-slice_fusion.2
  283.6 27.0 %fusion.5 = f32[1024,8192]{1,0:T(8,128)} fusion(f32[1024,8192]{1,0:T(8,128)} %get-tuple-element.204, bf16[2,1024,8192]{2,1,0:T(8,128)(2,1)} %get-tuple-element.216, s32[]{:T(128)} %get-tuple-element.203, f32[]{:T(128)} %bitcast.22, pred[]{:T(512)S(6)} %compare.3, pred[]{:T(512)} %lt.22), kind=kLoop, calls=%fused_computation.1.clone.1 | loop fusion | flops 41943040 | bytes 83886088 | tf_op jit(solution)/shard_map/while/body/eval_jaxpr/jit(_where)/select_n | solution.py:25
  310.6 43.1 %add_bitcast_fusion = f32[1,1024,8192]{2,1,0:T(8,128)} fusion(f32[1024,8192]{1,0:T(8,128)} %get-tuple-element.157, f32[1024,8192]{1,0:T(8,128)} %get-tuple-element.115, f32[1024,8192]{1,0:T(8,128)} %param.5, f32[]{:T(128)} %bitcast.3), kind=kLoop, calls=%fused_computation.3 | loop fusion | flops 33554432 | bytes 134217728 | tf_op jit(solution)/shard_map/broadcast_in_dim | solution.py:54
  (3 shorter events, 0.0 us)
Async XLA Ops:
  6.5 181.9 %all-gather.4.cloned.1.call-start = ((), (), s32[]{:S(2)}) async-start(), calls=%async_computation | async-start | bytes 14155776 | tf_op jit(solution)/shard_map/all_gather | solution.py:49
  9.5 203.6 %copy-start = (u32[32]{0:T(128)S(1)}, u32[32]{0:T(128)}, u32[]{:S(2)}) copy-start(u32[32]{0:T(128)} %constant.48) | copy-start | bytes 388
  9.5 252.9 %all-gather.6.cloned.1.call-start = ((), (), s32[]{:S(2)}) async-start(), calls=%async_computation.1 | async-start | bytes 50331648 | tf_op jit(solution)/shard_map/all_gather | solution.py:10
Sparse Core Ops, SparseCore 0:
  9.6 178.8 all-gather.3
  213.2 49.1 all-gather.5
where the time goes:
time: 361 us
  waiting for transfers between devices  225 us (62%)
  other arithmetic  91.9 us (25%)
  matrix products  24.6 us (7%)
  between operations  13.4 us (4%)
    all_gather x1, waiting for transfers between devices, local(): lax.all_gather(scaled, 'assets', axis=1, tiled=True)  179 us
    select_n x2, other arithmetic, turn(): return jax.tree.map(lambda a, b: jnp.where(reached, a, b), new, before)  45.9 us
    all_gather x1, waiting for transfers between devices, prefix(): lax.all_gather(part.astype(kind), axis)  45.6 us
    broadcast_in_dim x1, other arithmetic, local(): return result[None]  43.1 us
    dot_general x1, matrix products, cross_tile(): lax.dot_general(left, right, (((0,), (0,)), ((), ())), preferred_element_...  24.6 us
  transfers between devices with their start and end apart: 2, of which 2 were waited for; matrix products, arithmetic and copies ran while one was open for 0% of the time, Pallas kernels for 0%

commit v1 on v0

--- a/solution.py
+++ b/solution.py
@@ -46,7 +46,7 @@
     )
     factor = jnp.power(lam, jnp.float32(minutes))
     scaled = (returns.astype(jnp.float32) * weight[:, None]).astype(jnp.bfloat16)
-    tile = cross_tile(scaled, lax.all_gather(scaled, "assets", axis=1, tiled=True))
+    tile = cross_tile(scaled, jnp.concatenate(lax.all_gather(scaled, "assets"), axis=1))
     decay = jnp.full((1,), factor, jnp.float32)
     identity = (jnp.zeros_like(tile), jnp.ones((1,), jnp.float32))
     before, reach = prefix((tile, decay), "tm", combine_carry, identity)

time: 361 us -> 378 us (1.047)
  local copies, waits for them, and re-layouts: 2.47 us -> 19.1 us
    reshape x0 -> x1, local copies, waits for them, and re-layouts: none -> 16.7 us  [local(): jnp.concatenate(lax.all_gather(scaled, 'assets'), axis=1)]
where the time goes in v1:
time: 378 us; the launch traced here: 377 us
  waiting for transfers between devices  225 us (60%)
  other arithmetic  92 us (24%)
  matrix products  24.6 us (7%)
  local copies, waits for them, and re-layouts  19.1 us (5%)
  between operations  13.4 us (4%)
    all_gather x1, waiting for transfers between devices, local(): lax.all_gather(scaled, 'assets')  179 us
    select_n x2, other arithmetic, turn(): return jax.tree.map(lambda a, b: jnp.where(reached, a, b), new, before)  45.9 us
    all_gather x1, waiting for transfers between devices, prefix(): lax.all_gather(part.astype(kind), axis)  45.6 us
    broadcast_in_dim x1, other arithmetic, local(): return result[None]  43.1 us
    dot_general x1, matrix products, cross_tile(): lax.dot_general(left, right, (((0,), (0,)), ((), ())), preferred_element_...  24.6 us
    reshape x1, local copies, waits for them, and re-layouts, local(): jnp.concatenate(lax.all_gather(scaled, 'assets'), axis=1)  16.7 us
  transfers between devices with their start and end apart: 2, of which 2 were waited for; matrix products, arithmetic and copies ran while one was open for 0% of the time, Pallas kernels for 0%

profile of v1, /device:TPU:0, one launch (start us, length us, event | category | flops | bytes accessed | tf_op | source)
XLA Modules:
  0.0 377.3 jit_solution(7570115474438580902)
XLA Ops:
  6.5 0.0 all-gather.5.cloned.1.call-start
  6.6 3.0 multiply_convert_fusion
  9.5 0.0 all-gather.5.cloned.1.call-update
  9.5 0.0 all-gather.7.cloned.1.call-start
  9.6 178.9 %all-gather.5.cloned.1.call-done = bf16[6144,1024]{1,0:T(8,128)(2,1)} async-done(((bf16[768,1024]{1,0:T(8,128)(2,1)}), bf16[6144,1024]{1,0:T(8,128)(2,1)}) %all-gather.5.cloned.1.call-update) | async-done | bytes 12582928 | tf_op jit(solution)/shard_map/all_gather | solution.py:49
  188.5 16.7 %copy.5 = bf16[768,8,1024]{0,2,1:T(8,128)(2,1)} copy(bf16[768,8,1024]{2,0,1:T(8,128)(2,1)} %bitcast.30) | data formatting | bytes 25165824 | tf_op jit(solution)/shard_map/reshape | solution.py:49
  205.2 0.0 copy-start
  205.2 24.6 %fusion.1 = (bf16[1024,8192]{1,0:T(8,128)(2,1)}, f32[1024,8192]{1,0:T(8,128)}) fusion(bf16[768,1024]{1,0:T(8,128)(2,1)} %multiply_convert_fusion, bf16[768,8192]{0,1:T(8,128)(2,1)} %bitcast.31), kind=kOutput, calls=%fused_computation.6 | convolution fusion | flops 12893290496 | bytes 64487424 | tf_op jit(solution)/shard_map/dot_general | solution.py:31
  229.7 0.0 all-gather.7.cloned.1.call-update
  229.8 0.0 copy-done
  229.8 0.6 dynamic-slice
  230.4 0.7 dynamic-update-slice
  231.1 2.4 all-reduce
  233.6 45.6 %all-gather.7.cloned.1.call-done = bf16[2048,8192]{1,0:T(8,128)(2,1)} async-done(((bf16[1024,8192]{1,0:T(8,128)(2,1)}), bf16[2048,8192]{1,0:T(8,128)(2,1)}) %all-gather.7.cloned.1.call-update) | async-done | bytes 33554448 | tf_op jit(solution)/shard_map/all_gather | solution.py:10
  279.1 48.2 %while.16 = (s32[]{:T(128)}, f32[1024,8192]{1,0:T(8,128)}, f32[1]{0:T(128)}, s32[]{:T(128)}, bf16[2,1]{0,1:T(2,128)(2,1)S(1)}, /*index=5*/bf16[2,1024,8192]{2,1,0:T(8,128)(2,1)}, s32[]{:T(128)}, s32[]{:T(128)}) while((s32[]{:T(128)}, f32[1024,8192]{1,0:T(8,128)}, f32[1]{0:T(128)}, s32[]{:T(128)}, bf16[2,1]{0,1:T(2,128)(2,1)S(1)}, ...), condition=%wide.region_1.2_spmd.clone, body=%wide.region_0.1_spmd.clone.sunk | while | flops 41943044 | bytes 83886232 | solution.py:27
  279.1 0.6 constant_dynamic-slice_fusion.2
  280.3 18.9 %fusion.5 = f32[1024,8192]{1,0:T(8,128)} fusion(f32[1024,8192]{1,0:T(8,128)} %get-tuple-element.216, bf16[2,1024,8192]{2,1,0:T(8,128)(2,1)} %get-tuple-element.228, s32[]{:T(128)} %get-tuple-element.215, f32[]{:T(128)} %bitcast.26, pred[]{:T(512)S(6)} %compare.3, pred[]{:T(512)} %lt.22), kind=kLoop, calls=%fused_computation.1.clone.1 | loop fusion | flops 41943040 | bytes 83886088 | tf_op jit(solution)/shard_map/while/body/eval_jaxpr/jit(_where)/select_n | solution.py:25
  299.1 0.6 constant_dynamic-slice_fusion.2
  300.3 27.0 %fusion.5 = f32[1024,8192]{1,0:T(8,128)} fusion(f32[1024,8192]{1,0:T(8,128)} %get-tuple-element.216, bf16[2,1024,8192]{2,1,0:T(8,128)(2,1)} %get-tuple-element.228, s32[]{:T(128)} %get-tuple-element.215, f32[]{:T(128)} %bitcast.26, pred[]{:T(512)S(6)} %compare.3, pred[]{:T(512)} %lt.22), kind=kLoop, calls=%fused_computation.1.clone.1 | loop fusion | flops 41943040 | bytes 83886088 | tf_op jit(solution)/shard_map/while/body/eval_jaxpr/jit(_where)/select_n | solution.py:25
  327.3 43.1 %add_bitcast_fusion = f32[1,1024,8192]{2,1,0:T(8,128)} fusion(f32[1024,8192]{1,0:T(8,128)} %get-tuple-element.169, f32[1024,8192]{1,0:T(8,128)} %get-tuple-element.115, f32[1024,8192]{1,0:T(8,128)} %param.5, f32[]{:T(128)} %bitcast.6), kind=kLoop, calls=%fused_computation.3 | loop fusion | flops 33554432 | bytes 134217728 | tf_op jit(solution)/shard_map/broadcast_in_dim | solution.py:54
  (3 shorter events, 0.0 us)
Async XLA Ops:
  6.5 182.0 %all-gather.5.cloned.1.call-start = ((), (), s32[]{:S(2)}) async-start(), calls=%async_computation | async-start | bytes 14155776 | tf_op jit(solution)/shard_map/all_gather | solution.py:49
  9.5 269.6 %all-gather.7.cloned.1.call-start = ((), (), s32[]{:S(2)}) async-start(), calls=%async_computation.1 | async-start | bytes 50331648 | tf_op jit(solution)/shard_map/all_gather | solution.py:10
  205.2 24.6 %copy-start = (u32[32]{0:T(128)S(1)}, u32[32]{0:T(128)}, u32[]{:S(2)}) copy-start(u32[32]{0:T(128)} %constant.48) | copy-start | bytes 388
Sparse Core Ops, SparseCore 0:
  9.7 178.8 all-gather.4
  229.9 49.1 all-gather.6
